TPU v7x, 32 devices: a whole 2x2x4 slice. The times are simulated.
32 devices in a mesh: fsdp: 4 (over y, x), seq: 8 (over z, core).
Axes of the slice: x: 2, y: 2, z: 4, core: 2. Of those that a mesh axis runs over, the one named last changes fastest.
Arguments:
- images: bfloat16 [32, 1024, 1152], P('fsdp', 'seq'), may hold values from -8 to 8
- lengths: int32 [32], P('fsdp'), may hold values from 256 to 1024
- ln1_gain: bfloat16 [1152], P('fsdp'), may hold values from 0.099609375 to 1.8984375
- ln1_bias: bfloat16 [1152], P('fsdp'), may hold values from -3 to 3
- w_qkv: bfloat16 [1152, 3456], P('fsdp'), may hold values from -1 to 1
- qv_bias: bfloat16 [2, 1152], P(None, 'fsdp'), may hold values from -3 to 3
- w_out: bfloat16 [1152, 1152], P('fsdp'), may hold values from -0.75 to 0.75
- out_bias: bfloat16 [1152], P('fsdp'), may hold values from -3 to 3
- ln2_gain: bfloat16 [1152], P('fsdp'), may hold values from 0.099609375 to 1.8984375
- ln2_bias: bfloat16 [1152], P('fsdp'), may hold values from -3 to 3
- w_up: bfloat16 [1152, 4304], P('fsdp'), may hold values from -0.1875 to 0.1875
- up_bias: bfloat16 [4304], P('fsdp'), may hold values from -3 to 3
- w_down: bfloat16 [4304, 1152], P(None, 'fsdp'), may hold values from -0.09375 to 0.09375
- down_bias: bfloat16 [1152], P('fsdp'), may hold values from -3 to 3
- cotangent: bfloat16 [32, 1024, 1152], P('fsdp', 'seq'), may hold values from -6 to 6
Outputs:
- layer_out: bfloat16 [32, 1024, 1152], P('fsdp', 'seq')
- grad_images: bfloat16 [32, 1024, 1152], P('fsdp', 'seq')
- grad_ln1_gain: float32 [1152], P('fsdp')
- grad_ln1_bias: float32 [1152], P('fsdp')
- grad_w_qkv: float32 [1152, 3456], P('fsdp')
- grad_qv_bias: float32 [2, 1152], P(None, 'fsdp')
- grad_w_out: float32 [1152, 1152], P('fsdp')
- grad_out_bias: float32 [1152], P('fsdp')
- grad_ln2_gain: float32 [1152], P('fsdp')
- grad_ln2_bias: float32 [1152], P('fsdp')
- grad_w_up: float32 [1152, 4304], P('fsdp')
- grad_up_bias: float32 [4304], P('fsdp')
- grad_w_down: float32 [4304, 1152], P(None, 'fsdp')
- grad_down_bias: float32 [1152], P('fsdp')
All inputs are finite; a program needn't handle non-finite values.
Results may differ from a plain program's by a relative error of at most 0.017.
Values may be sent and summed in bfloat16 or wider, within the bound.
A program may use at most 256 MiB of HBM per device.

v0:
```python
import jax
import jax.numpy as jnp
from jax import lax
from jax.sharding import PartitionSpec as P

H = 16
HD = 72
epsilon = 1e-06
wide_block = 1024


def for_sending(shard):

    def short(part):
        return part.astype(jnp.bfloat16) if part.dtype == jnp.float32 else part

    return jax.tree.map(short, shard)


def normalize(field, gain_vec, bias_vec):
    center_mean = jnp.mean(field, -1, keepdims=True)
    centered = field - center_mean
    variance = jnp.mean(centered * centered, -1, keepdims=True)
    return centered * lax.rsqrt(variance + epsilon) * gain_vec + bias_vec


def gelu_tanh(field):
    return jax.nn.gelu(field, approximate=True)


def attend_item(queries, keys_all, values, length_one):
    length_all = keys_all.shape[1]
    block_rows = min(wide_block, length_all)
    visible = (jnp.arange(length_all) < length_one)[None, :]
    pieces = []
    log_sums = []
    for offset in range(0, length_all, block_rows):
        scores = jnp.einsum(
            "dq,dk->qk",
            queries[:, offset : offset + block_rows],
            keys_all,
            preferred_element_type=jnp.float32,
        )
        scores = jnp.where(visible, scores, -1e30)
        row_max = jnp.max(scores, -1, keepdims=True)
        exponents = jnp.exp(scores - row_max)
        denominator = jnp.sum(exponents, -1, keepdims=True)
        softmax_low = (exponents / denominator).astype(jnp.bfloat16)
        pieces.append(
            jnp.einsum("qk,dk->dq", softmax_low, values, preferred_element_type=jnp.float32)
        )
        log_sums.append(row_max[:, 0] + jnp.log(denominator[:, 0]))
    return (jnp.concatenate(pieces, 1).astype(jnp.bfloat16), jnp.concatenate(log_sums, 0))


def attend_back(queries, keys_all, values, length_one, log_sum, grad_mixed):
    length_all = keys_all.shape[1]
    block_rows = min(wide_block, length_all)
    visible = (jnp.arange(length_all) < length_one)[None, :]
    grad_keys = jnp.zeros(keys_all.shape, jnp.float32)
    grad_values = jnp.zeros(values.shape, jnp.float32)
    grad_pieces = []
    for offset in range(0, length_all, block_rows):
        query_rows = queries[:, offset : offset + block_rows]
        grad_rows = grad_mixed[:, offset : offset + block_rows]
        scores = jnp.einsum("dq,dk->qk", query_rows, keys_all, preferred_element_type=jnp.float32)
        scores = jnp.where(visible, scores, -1e30)
        softmax_out = jnp.exp(scores - log_sum[offset : offset + block_rows, None])
        grad_soft = jnp.einsum("dq,dk->qk", grad_rows, values, preferred_element_type=jnp.float32)
        row_dot = jnp.sum(softmax_out * grad_soft, -1, keepdims=True)
        grad_scores = (softmax_out * (grad_soft - row_dot)).astype(jnp.bfloat16)
        grad_pieces.append(
            jnp.einsum("qk,dk->dq", grad_scores, keys_all, preferred_element_type=jnp.float32)
        )
        grad_keys = grad_keys + jnp.einsum(
            "qk,dq->dk", grad_scores, query_rows, preferred_element_type=jnp.float32
        )
        grad_values = grad_values + jnp.einsum(
            "qk,dq->dk",
            softmax_out.astype(jnp.bfloat16),
            grad_rows,
            preferred_element_type=jnp.float32,
        )
    return (
        jnp.concatenate(grad_pieces, 1).astype(jnp.bfloat16),
        grad_keys.astype(jnp.bfloat16),
        grad_values.astype(jnp.bfloat16),
    )


def on_device(
    images,
    lengths,
    ln1_gain,
    ln1_bias,
    w_qkv,
    qv_bias,
    w_out,
    out_bias,
    ln2_gain,
    ln2_bias,
    w_up,
    up_bias,
    w_down,
    down_bias,
    cotangent,
):
    image_count, token_count, width_all = images.shape
    head_scale = HD ** (-0.5)
    gain_first, bias_first, qkv_full, qv_full, out_full, outb_full = (
        lax.all_gather(ln1_gain, "fsdp", axis=0, tiled=True),
        lax.all_gather(ln1_bias, "fsdp", axis=0, tiled=True),
        lax.all_gather(w_qkv, "fsdp", axis=0, tiled=True),
        lax.all_gather(qv_bias, "fsdp", axis=1, tiled=True),
        lax.all_gather(w_out, "fsdp", axis=0, tiled=True),
        lax.all_gather(out_bias, "fsdp", axis=0, tiled=True),
    )
    inputs_all = images.astype(jnp.float32)
    normed_first, norm_first_back = jax.vjp(
        normalize, inputs_all, gain_first.astype(jnp.float32), bias_first.astype(jnp.float32)
    )
    normed_attn = normed_first.astype(jnp.bfloat16)
    qkv_split = qkv_full.reshape(width_all, 3, H, HD)
    projected = jnp.einsum(
        "itd,dahe->ahiet", normed_attn, qkv_split, preferred_element_type=jnp.float32
    )
    shift_pair = qv_full.astype(jnp.float32).reshape(2, H, HD)
    queries = (projected[0] + shift_pair[0][:, None, :, None]) * head_scale
    values = projected[2] + shift_pair[1][:, None, :, None]
    stacked = jnp.stack([queries, projected[1], values]).astype(jnp.bfloat16)
    head_view = lax.all_to_all(stacked, "seq", split_axis=1, concat_axis=4, tiled=True)
    local_heads = head_view.shape[1]
    item_count = local_heads * image_count
    query_items = head_view[0].reshape(item_count, HD, -1)
    key_items = head_view[1].reshape(item_count, HD, -1)
    value_items = head_view[2].reshape(item_count, HD, -1)
    item_lengths = jnp.tile(lengths, local_heads)
    mixed_items, log_sums = lax.map(
        lambda packed: attend_item(*packed), (query_items, key_items, value_items, item_lengths)
    )
    mixed_tokens = lax.all_to_all(
        for_sending(mixed_items.reshape(local_heads, image_count, HD, -1)),
        "seq",
        split_axis=3,
        concat_axis=0,
        tiled=True,
    )
    out_split = out_full.reshape(H, HD, width_all)
    residual = (
        inputs_all
        + jnp.einsum("hiet,hed->itd", mixed_tokens, out_split, preferred_element_type=jnp.float32)
        + outb_full.astype(jnp.float32)
    )
    gain_second, bias_second, up_full, upb_full, down_full, downb_full = (
        lax.all_gather(ln2_gain, "fsdp", axis=0, tiled=True),
        lax.all_gather(ln2_bias, "fsdp", axis=0, tiled=True),
        lax.all_gather(w_up, "fsdp", axis=0, tiled=True),
        lax.all_gather(up_bias, "fsdp", axis=0, tiled=True),
        lax.all_gather(w_down, "fsdp", axis=1, tiled=True),
        lax.all_gather(down_bias, "fsdp", axis=0, tiled=True),
    )
    normed_second, norm_second_back = jax.vjp(
        normalize, residual, gain_second.astype(jnp.float32), bias_second.astype(jnp.float32)
    )
    normed_mlp = normed_second.astype(jnp.bfloat16)
    pre_act = jnp.einsum(
        "itd,df->itf", normed_mlp, up_full, preferred_element_type=jnp.float32
    ) + upb_full.astype(jnp.float32)
    activation, gelu_back = jax.vjp(gelu_tanh, pre_act)
    activation = activation.astype(jnp.bfloat16)
    output_all = (
        residual
        + jnp.einsum("itf,fd->itd", activation, down_full, preferred_element_type=jnp.float32)
        + downb_full.astype(jnp.float32)
    )
    layer_out = output_all.astype(jnp.bfloat16)
    qkv_back, out_back = (
        lax.all_gather(w_qkv, "fsdp", axis=0, tiled=True),
        lax.all_gather(w_out, "fsdp", axis=0, tiled=True),
    )
    up_back, down_back = (
        lax.all_gather(w_up, "fsdp", axis=0, tiled=True),
        lax.all_gather(w_down, "fsdp", axis=1, tiled=True),
    )
    grad_down = jnp.einsum("itf,itd->fd", activation, cotangent, preferred_element_type=jnp.float32)
    grad_downb = jnp.sum(cotangent, axis=(0, 1), dtype=jnp.float32)
    grad_act = jnp.einsum("itd,fd->itf", cotangent, down_back, preferred_element_type=jnp.float32)
    (grad_pre,) = gelu_back(grad_act)
    grad_pre = grad_pre.astype(jnp.bfloat16)
    grad_up = jnp.einsum("itd,itf->df", normed_mlp, grad_pre, preferred_element_type=jnp.float32)
    grad_upb = jnp.sum(grad_pre, axis=(0, 1), dtype=jnp.float32)
    grad_normed_mlp = jnp.einsum(
        "itf,df->itd", grad_pre, up_back, preferred_element_type=jnp.float32
    )
    grad_resid_norm, grad_gain_second, grad_bias_second = norm_second_back(grad_normed_mlp)
    grad_residual = cotangent.astype(jnp.float32) + grad_resid_norm
    grad_branch = grad_residual.astype(jnp.bfloat16)
    grad_outw = jnp.einsum(
        "hiet,itd->hed", mixed_tokens, grad_branch, preferred_element_type=jnp.float32
    ).reshape(width_all, width_all)
    grad_outb = jnp.sum(grad_branch, axis=(0, 1), dtype=jnp.float32)
    out_back_split = out_back.reshape(H, HD, width_all)
    grad_mixed = jnp.einsum(
        "itd,hed->hiet", grad_branch, out_back_split, preferred_element_type=jnp.float32
    ).astype(jnp.bfloat16)
    grad_head_view = lax.all_to_all(grad_mixed, "seq", split_axis=0, concat_axis=3, tiled=True)
    grad_items = grad_head_view.reshape(item_count, HD, -1)
    grad_q, grad_k, grad_v = lax.map(
        lambda packed: attend_back(*packed),
        (query_items, key_items, value_items, item_lengths, log_sums, grad_items),
    )
    grad_stack = jnp.stack([grad_q, grad_k, grad_v]).reshape(3, local_heads, image_count, HD, -1)
    grad_projected = lax.all_to_all(
        for_sending(grad_stack), "seq", split_axis=4, concat_axis=1, tiled=True
    ).astype(grad_stack.dtype)
    column_scales = jnp.array([head_scale, 1.0, 1.0], jnp.float32)
    grad_qkv = (
        jnp.einsum(
            "itd,ahiet->dahe", normed_attn, grad_projected, preferred_element_type=jnp.float32
        )
        * column_scales[None, :, None, None]
    ).reshape(width_all, 3 * width_all)
    shift_sums = jnp.sum(grad_projected, axis=(2, 4), dtype=jnp.float32)
    grad_qvb = jnp.stack([shift_sums[0] * head_scale, shift_sums[2]]).reshape(2, width_all)
    qkv_back_split = qkv_back.reshape(width_all, 3, H, HD)
    grad_normed_attn = head_scale * jnp.einsum(
        "hiet,dhe->itd", grad_projected[0], qkv_back_split[:, 0], preferred_element_type=jnp.float32
    )
    grad_normed_attn = grad_normed_attn + jnp.einsum(
        "ahiet,dahe->itd",
        grad_projected[1:],
        qkv_back_split[:, 1:],
        preferred_element_type=jnp.float32,
    )
    grad_input_norm, grad_gain_first, grad_bias_first = norm_first_back(grad_normed_attn)
    grad_images = (grad_residual + grad_input_norm).astype(jnp.bfloat16)
    (
        part_gone,
        part_bone,
        part_qkv,
        part_qvb,
        part_outw,
        part_outb,
        part_gtwo,
        part_btwo,
        part_up,
        part_upb,
        part_down,
        part_downb,
    ) = (
        lax.psum_scatter(
            grad_gain_first.astype(jnp.bfloat16), "fsdp", scatter_dimension=0, tiled=True
        ).astype(jnp.float32),
        lax.psum_scatter(
            grad_bias_first.astype(jnp.bfloat16), "fsdp", scatter_dimension=0, tiled=True
        ).astype(jnp.float32),
        lax.psum_scatter(
            grad_qkv.astype(jnp.bfloat16), "fsdp", scatter_dimension=0, tiled=True
        ).astype(jnp.float32),
        lax.psum_scatter(
            grad_qvb.astype(jnp.bfloat16), "fsdp", scatter_dimension=1, tiled=True
        ).astype(jnp.float32),
        lax.psum_scatter(
            grad_outw.astype(jnp.bfloat16), "fsdp", scatter_dimension=0, tiled=True
        ).astype(jnp.float32),
        lax.psum_scatter(
            grad_outb.astype(jnp.bfloat16), "fsdp", scatter_dimension=0, tiled=True
        ).astype(jnp.float32),
        lax.psum_scatter(
            grad_gain_second.astype(jnp.bfloat16), "fsdp", scatter_dimension=0, tiled=True
        ).astype(jnp.float32),
        lax.psum_scatter(
            grad_bias_second.astype(jnp.bfloat16), "fsdp", scatter_dimension=0, tiled=True
        ).astype(jnp.float32),
        lax.psum_scatter(
            grad_up.astype(jnp.bfloat16), "fsdp", scatter_dimension=0, tiled=True
        ).astype(jnp.float32),
        lax.psum_scatter(
            grad_upb.astype(jnp.bfloat16), "fsdp", scatter_dimension=0, tiled=True
        ).astype(jnp.float32),
        lax.psum_scatter(
            grad_down.astype(jnp.bfloat16), "fsdp", scatter_dimension=1, tiled=True
        ).astype(jnp.float32),
        lax.psum_scatter(
            grad_downb.astype(jnp.bfloat16), "fsdp", scatter_dimension=0, tiled=True
        ).astype(jnp.float32),
    )
    (
        final_gone,
        final_bone,
        final_qkv,
        final_qvb,
        final_outw,
        final_outb,
        final_gtwo,
        final_btwo,
        final_up,
        final_upb,
        final_down,
        final_downb,
    ) = (
        lax.psum(part_gone.astype(jnp.bfloat16), "seq").astype(jnp.float32),
        lax.psum(part_bone.astype(jnp.bfloat16), "seq").astype(jnp.float32),
        lax.psum(part_qkv.astype(jnp.bfloat16), "seq").astype(jnp.float32),
        lax.psum(part_qvb.astype(jnp.bfloat16), "seq").astype(jnp.float32),
        lax.psum(part_outw.astype(jnp.bfloat16), "seq").astype(jnp.float32),
        lax.psum(part_outb.astype(jnp.bfloat16), "seq").astype(jnp.float32),
        lax.psum(part_gtwo.astype(jnp.bfloat16), "seq").astype(jnp.float32),
        lax.psum(part_btwo.astype(jnp.bfloat16), "seq").astype(jnp.float32),
        lax.psum(part_up.astype(jnp.bfloat16), "seq").astype(jnp.float32),
        lax.psum(part_upb.astype(jnp.bfloat16), "seq").astype(jnp.float32),
        lax.psum(part_down.astype(jnp.bfloat16), "seq").astype(jnp.float32),
        lax.psum(part_downb.astype(jnp.bfloat16), "seq").astype(jnp.float32),
    )
    return (
        layer_out,
        grad_images,
        final_gone,
        final_bone,
        final_qkv,
        final_qvb,
        final_outw,
        final_outb,
        final_gtwo,
        final_btwo,
        final_up,
        final_upb,
        final_down,
        final_downb,
    )


def solution(mesh):
    placed = (
        P("fsdp", "seq", None),
        P("fsdp"),
        P("fsdp"),
        P("fsdp"),
        P("fsdp", None),
        P(None, "fsdp"),
        P("fsdp", None),
        P("fsdp"),
        P("fsdp"),
        P("fsdp"),
        P("fsdp", None),
        P("fsdp"),
        P(None, "fsdp"),
        P("fsdp"),
        P("fsdp", "seq", None),
    )
    return jax.shard_map(
        on_device,
        mesh=mesh,
        in_specs=placed,
        out_specs=(
            P("fsdp", "seq", None),
            P("fsdp", "seq", None),
            P("fsdp"),
            P("fsdp"),
            P("fsdp", None),
            P(None, "fsdp"),
            P("fsdp", None),
            P("fsdp"),
            P("fsdp"),
            P("fsdp"),
            P("fsdp", None),
            P("fsdp"),
            P(None, "fsdp"),
            P("fsdp"),
        ),
        check_vma=False,
    )
```

profile of v0, /device:TPU:0, one launch (start us, length us, event | category | flops | bytes accessed | tf_op | source)
XLA Modules:
  0.0 1667.9 jit_solution(1936642603031009704)
XLA Ops:
  13.0 18.5 %all-reduce.17 = (bf16[1152]{0:T(1024)(128)(2,1)S(1)}, bf16[1152]{0:T(1024)(128)(2,1)S(1)}, bf16[1152]{0:T(1024)(128)(2,1)S(1)}, bf16[1152]{0:T(1024)(128)(2,1)S...) all-reduce(bf16[1152]{0:T(1024)(128)(2,1)S(1)} %dynamic-update-slic, ...), channel_id=1, replica_groups=mesh['fsdp'=4,'seq'=8] {'fsdp'}, use_global_device_ids=true, to_apply=%add.1 | all-reduce | flops 10064 | bytes 40256
  41.1 55.8 %all-gather.6.cloned.1.call-done = bf16[1152,3456]{1,0:T(8,128)(2,1)} async-done(((bf16[288,3456]{1,0:T(8,128)(2,1)}), bf16[1152,3456]{1,0:T(8,128)(2,1)}) %all-gather.6.cloned.1.call-update) | async-done | bytes 7962640 | tf_op jit(solution)/shard_map/all_gather | solution.py:113
  96.9 11.5 copy.97
  108.5 12.5 convolution_bitcast_fusion.3
  133.9 155.1 %all-to-all-done = bf16[3,16,8,72,128]{4,3,0,2,1:T(8,128)(2,1)} async-done(((bf16[3,16,8,72,128]{4,3,0,2,1:T(8,128)(2,1)}), bf16[3,16,8,72,128]{4,3,0,2,1:T(8,128)(2,1)}, u32[]{:S(2)}, u32[]{:S(2)}) %all-to-all-start) | async-done | bytes 7077920 | tf_op jit(solution)/shard_map/all_to_all | solution.py:131
  325.3 180.0 %while.26 = (s32[]{:T(128)}, bf16[16,72,1024]{2,1,0:T(8,128)(2,1)}, f32[16,1024]{1,0:T(8,128)}, bf16[16,72,1024]{2,1,0:T(8,128)(2,1)}, s32[16]{0:T(128)S(1)}, /*...) while((s32[]{:T(128)}, bf16[16,72,1024]{2,1,0:T(8,128)(2,1)}, ...), condition=%wide.region_5.6_spmd, body=%wide.region_2.5_spmd.sunk | while | flops 311500800 | bytes 29997196 | solution.py:138
  516.7 93.5 %all-to-all-done.1 = bf16[2,8,72,1024]{2,1,0,3:T(8,128)(2,1)} async-done(((bf16[2,8,72,1024]{2,1,0,3:T(8,128)(2,1)}), bf16[2,8,72,1024]{2,1,0,3:T(8,128)(2,1)}, u32[]{:S(2)}, u32[]{:S(2)}) %all-to-all-start.1) | async-done | bytes 2359328 | tf_op jit(solution)/shard_map/all_to_all | solution.py:141
  625.9 24.8 %multiply_convert_fusion.1 = (bf16[8,128,4304]{1,2,0:T(8,128)(2,1)}, f32[8,128,4304]{1,2,0:T(8,128)}) fusion(f32[4304]{0:T(1024)S(1)} %convert_element_type.186, bf16[1152,4304]{1,0:T(8,128)(2,1)} %all-gather.10.cloned.1.call-done, f32[8,128,1152]{2,1,0:T(8,128)} %copy-done.5, f32[1152]{0:T(1024)S(1)} %convert_element_type.184, ...), kind=kOutput, calls=%fused_computation.72 | convolution fusion | flops 10204381184 | bytes 41113408 | tf_op jit(solution)/shard_map/itd,df->itf/dot_general | solution.py:166
  650.7 32.5 %fusion.117 = (bf16[4304]{0:T(1024)(128)(2,1)}, bf16[8,128,4304]{1,2,0:T(8,128)(2,1)}) fusion(f32[8,128,4304]{1,2,0:T(8,128)} %get-tuple-element.199, f32[4304]{0:T(1024)S(1)} %convert_element_type.186, bf16[8,128,1152]{2,1,0:T(8,128)(2,1)} %param.34, bf16[4304,1152]{0,1:T(8,128)(2,1)} %all-gather.12.cloned.1.call-done), kind=kOutput, calls=%fused_computation.155 | convolution fusion | flops 10251366400 | bytes 38745312 | tf_op jit(solution)/shard_map/itd,fd->itf/dot_general | solution.py:187
  683.2 20.6 %multiply_reduce_fusion.1 = (bf16[1152]{0:T(1024)(128)(2,1)}, f32[8,128]{1,0:T(8,128)S(1)}, bf16[1152]{0:T(1024)(128)(2,1)}, f32[8,128,1152]{2,1,0:T(8,128)}) fusion(f32[8,128,1152]{2,1,0:T(8,128)S(1)} %bitcast.254, f32[8,128]{1,0:T(8,128)S(1)} %fusion.109, f32[8,128]{1,0:T(8,128)S(1)} %broadcast_multiply_fusion, f32[1152]{0:T(1024)S(1)} %convert_element_type.183, ...), kind=kOutput, calls=%fused_computation.117 | convolution fusion | flops 10163844096 | bytes 28189696 | tf_op jit(solution)/shard_map/itf,df->itd/dot_general | solution.py:192
  715.4 19.1 %fusion.54 = bf16[1152,4304]{1,0:T(8,128)(2,1)} fusion(bf16[8,128,4304]{1,2,0:T(8,128)(2,1)} %get-tuple-element.203, f32[8,128,1152]{2,1,0:T(8,128)} %copy-done.5, f32[1152]{0:T(1024)S(1)} %convert_element_type.184, f32[1152]{0:T(1024)S(1)} %convert_element_type.183, f32[8,128]{1,0:T(8,128)S(1)} %fusion.109, f32[8,128]{1,0:T(8,128)S(1)} %broadcast_multiply_fusion), kind=kOutput, calls=%fused_computation.63 | convolution fusion | flops 10165266432 | bytes 23467008 | tf_op jit(solution)/shard_map/itd,itf->df/dot_general | solution.py:190
  747.3 16.5 fusion.55
  764.1 37.8 %all-to-all-done.2 = bf16[16,8,72,128]{3,2,1,0:T(8,128)(2,1)} async-done(((bf16[16,8,72,128]{3,2,1,0:T(8,128)(2,1)}), bf16[16,8,72,128]{3,2,1,0:T(8,128)(2,1)}, u32[]{:S(2)}, u32[]{:S(2)}) %all-to-all-start.2) | async-done | bytes 2359328 | tf_op jit(solution)/shard_map/all_to_all | solution.py:206
  811.2 220.9 %while.27 = (s32[]{:T(128)}, bf16[16,72,1024]{2,1,0:T(8,128)(2,1)S(1)}, bf16[16,72,1024]{2,1,0:T(8,128)(2,1)}, bf16[16,72,1024]{2,1,0:T(8,128)(2,1)}, bf16[16,72...) while((s32[]{:T(128)}, ...), condition=%wide.region_12.13_spmd, body=%wide.region_10.12_spmd.sunk | while | flops 767778816 | bytes 32969856 | solution.py:208
  1056.7 277.4 %all_to_all.66 = bf16[3,2,8,72,1024]{3,2,1,0,4:T(8,128)(2,1)} all-to-all(bf16[3,2,8,72,1024]{3,2,1,0,4:T(8,128)(2,1)S(1)} %pad_maximum_fusion), channel_id=1, replica_groups=mesh['fsdp'=4,'seq'=8] {'seq'}, dimensions={4} | all-to-all | bytes 14155776 | tf_op jit(solution)/shard_map/all_to_all | solution.py:213
  1334.1 15.4 copy.114
  1349.5 13.9 fusion.63
  1363.4 11.6 copy.115
  1376.8 13.2 copy.133
  1424.5 17.1 %all-reduce.16 = (bf16[1152]{0:T(1024)(128)(2,1)S(1)}, bf16[1152]{0:T(1024)(128)(2,1)S(1)}, bf16[1152]{0:T(1024)(128)(2,1)S(1)}, bf16[1152]{0:T(1024)(128)(2,1)S...) all-reduce(bf16[1152]{0:T(1024)(128)(2,1)S(1)} %dynamic-update-slic, ...), channel_id=1, replica_groups=mesh['fsdp'=4,'seq'=8] {'fsdp'}, use_global_device_ids=true, to_apply=%add.6 | all-reduce | flops 12368 | bytes 49472
  1442.2 15.3 reduce-scatter.8.cloned.1.call-done
  1464.1 19.0 %fusion.94 = bf16[8,128,1152]{2,1,0:T(8,128)(2,1)} fusion(f32[8,128,1152]{2,1,0:T(8,128)} %copy-done.5, bf16[8,128,4304]{1,2,0:T(8,128)(2,1)} %get-tuple-element.198, bf16[4304,1152]{0,1:T(8,128)(2,1)} %all-gather.12.cloned.1.call-done, f32[1152]{0:T(1024)S(1)} %convert_element_type.188), kind=kOutput, calls=%fused_computation.123 | convolution fusion | flops 10157948928 | bytes 25813504 | tf_op jit(solution)/shard_map/itf,fd->itd/dot_general | solution.py:173
  1486.2 29.3 %all-reduce.14 = (bf16[288]{0:T(512)(128)(2,1)S(1)}, bf16[288]{0:T(512)(128)(2,1)S(1)}, bf16[2,288]{1,0:T(2,128)(2,1)S(1)}, bf16[288]{0:T(512)(128)(2,1)S(1)}, b...) all-reduce(bf16[288]{0:T(512)(128)(2,1)S(1)} %dynamic-slice.8, ...), channel_id=1, replica_groups=mesh['fsdp'=4,'seq'=8] {'seq'}, use_global_device_ids=true, to_apply=%region_17.18 | all-reduce | flops 3380 | bytes 13520 | tf_op jit(solution)/shard_map/psum | solution.py:302
  1520.2 130.0 %all-reduce.20.cloned.1.call-done = (bf16[288,3456]{1,0:T(8,128)(2,1)}, bf16[288,1152]{1,0:T(8,128)(2,1)}, bf16[288,4304]{1,0:T(8,128)(2,1)}, bf16[4304,288]{0,1:T(8,128)(2,1)}) async-done(((bf16[288,3456]{1,0:T(8,128)(2,1)}, bf16[288,1152]{1,0:T(8,128)(2,1)}, bf16[288,4304]{1,0:T(8,128)(2,1)}, bf16[4304,288]{0,1:T(8,128)(2,1)}), (bf16[288,3456]{1,0:T(8,128)(2,1)}, bf16[288,1152]{1,0:T(8,128)(2,1)}, ...) | async-done | bytes 7612432 | tf_op jit(solution)/shard_map/psum | solution.py:304
  (526 shorter events, 608.5 us)
Async XLA Ops:
  7.3 24.2 %copy-start.2 = (bf16[8,128,1152]{2,1,0:T(8,128)(2,1)S(1)}, bf16[8,128,1152]{2,1,0:T(8,128)(2,1)}, u32[]{:S(2)}) copy-start(bf16[8,128,1152]{2,1,0:T(8,128)(2,1)} %param.20) | copy-start | bytes 7077892
  7.3 26.0 %copy-start.34 = (bf16[2,288]{1,0:T(2,128)(2,1)S(1)}, bf16[2,288]{1,0:T(2,128)(2,1)}, u32[]{:S(2)}) copy-start(bf16[2,288]{1,0:T(2,128)(2,1)} %param.25) | copy-start | bytes 3460
  7.3 89.6 %all-gather.6.cloned.1.call-start = ((), (), s32[]{:S(2)}) async-start(), calls=%async_computation.9 | async-start | bytes 9953280 | tf_op jit(solution)/shard_map/all_gather | solution.py:113
  8.0 608.5 %all-gather.8.cloned.1.call-start = ((), (), s32[]{:S(2)}) async-start(), calls=%async_computation.10 | async-start | bytes 3317760 | tf_op jit(solution)/shard_map/all_gather | solution.py:115
  8.8 617.1 %all-gather.10.cloned.1.call-start = ((), (), s32[]{:S(2)}) async-start(), calls=%async_computation.11 | async-start | bytes 12533760 | tf_op jit(solution)/shard_map/all_gather | solution.py:157
  31.5 77.0 %copy-start.15 = (f32[1152]{0:T(1024)}, f32[1152]{0:T(1024)S(1)}, u32[]{:S(2)}) copy-start(f32[1152]{0:T(1024)S(1)} %convert_element_type.178) | copy-start | bytes 13828
  31.5 77.0 %copy-start.28 = (f32[1152]{0:T(1024)}, f32[1152]{0:T(1024)S(1)}, u32[]{:S(2)}) copy-start(f32[1152]{0:T(1024)S(1)} %convert_element_type.179) | copy-start | bytes 13828
  31.9 76.6 %copy-start.17 = (f32[8,128]{1,0:T(8,128)}, f32[8,128]{1,0:T(8,128)S(1)}, u32[]{:S(2)}) copy-start(f32[8,128]{1,0:T(8,128)S(1)} %broadcast_multiply_fusion.1) | copy-start | bytes 12292
  32.7 75.8 %copy-start.21 = (f32[8,128]{1,0:T(8,128)}, f32[8,128]{1,0:T(8,128)S(1)}, u32[]{:S(2)}) copy-start(f32[8,128]{1,0:T(8,128)S(1)} %fusion.108) | copy-start | bytes 12292
  128.3 160.7 %all-to-all-start = ((bf16[3,16,8,72,128]{4,3,0,2,1:T(8,128)(2,1)}), bf16[3,16,8,72,128]{4,3,0,2,1:T(8,128)(2,1)}, u32[]{:S(2)}, u32[]{:S(2)}) async-start(bf16[3,16,8,72,128]{4,3,0,2,1:T(8,128)(2,1)} %copy.99), calls=%async_computation | async-start | bytes 14155776 | tf_op jit(solution)/shard_map/all_to_all | solution.py:131
  133.2 517.4 %all-gather.12.cloned.1.call-start = ((), (), s32[]{:S(2)}) async-start(), calls=%async_computation.12 | async-start | bytes 12533760 | tf_op jit(solution)/shard_map/all_gather | solution.py:159
  511.7 98.5 %all-to-all-start.1 = ((bf16[2,8,72,1024]{2,1,0,3:T(8,128)(2,1)}), bf16[2,8,72,1024]{2,1,0,3:T(8,128)(2,1)}, u32[]{:S(2)}, u32[]{:S(2)}) async-start(bf16[2,8,72,1024]{2,1,0,3:T(8,128)(2,1)} %bitcast.255), calls=%async_computation.1 | async-start | bytes 8388608 | tf_op jit(solution)/shard_map/all_to_all | solution.py:141
  516.2 926.0 %reduce-scatter.10.cloned.1.call-start = ((), (), s32[]{:S(2)}) async-start(), calls=%async_computation.14 | async-start | bytes 3317760 | tf_op jit(solution)/shard_map/reduce_scatter | solution.py:263
  625.9 57.3 %slice-start = ((s8[4718592]{0:T(1024)(128)(4,1)}), s8[524288]{0:T(1024)(128)(4,1)S(1)}, s32[]{:S(2)}) async-start(s8[4718592]{0:T(1024)(128)(4,1)} %bitcast.253), calls=%async_computation.19 | async-start | bytes 1048576
  650.7 32.5 %slice-start.1 = ((s8[4718592]{0:T(1024)(128)(4,1)}), s8[4194304]{0:T(1024)(128)(4,1)S(1)}, s32[]{:S(2)}) async-start(s8[4718592]{0:T(1024)(128)(4,1)} %bitcast.253), calls=%async_computation.20 | async-start | bytes 8388608
  715.4 726.9 %reduce-scatter.12.cloned.1.call-start = ((), (), s32[]{:S(2)}) async-start(), calls=%async_computation.15 | async-start | bytes 12533760 | tf_op jit(solution)/shard_map/reduce_scatter | solution.py:275
  742.9 59.0 %all-to-all-start.2 = ((bf16[16,8,72,128]{3,2,1,0:T(8,128)(2,1)}), bf16[16,8,72,128]{3,2,1,0:T(8,128)(2,1)}, u32[]{:S(2)}, u32[]{:S(2)}) async-start(bf16[16,8,72,128]{3,2,1,0:T(8,128)(2,1)} %copy.106), calls=%async_computation.2 | async-start | bytes 4718592 | tf_op jit(solution)/shard_map/all_to_all | solution.py:206
  747.2 695.0 %reduce-scatter.14.cloned.1.call-start = ((), (), s32[]{:S(2)}) async-start(), calls=%async_computation.16 | async-start | bytes 12533760 | tf_op jit(solution)/shard_map/reduce_scatter | solution.py:281
  763.8 693.7 %reduce-scatter.8.cloned.1.call-start = ((), (), s32[]{:S(2)}) async-start(), calls=%async_computation.13 | async-start | bytes 9953280 | tf_op jit(solution)/shard_map/reduce_scatter | solution.py:257
  1334.0 15.4 copy-start.29
  1334.1 15.4 copy-start.44
  1375.0 110.2 %reduce-scatter.16.cloned.1.call-start = ((), (), s32[]{:S(2)}) async-start(), calls=%async_computation.17 | async-start | bytes 368640
  1420.4 229.8 %all-reduce.20.cloned.1.call-start = ((), (), s32[]{:S(2)}) async-start(), calls=%async_computation.18 | async-start | bytes 15335424 | tf_op jit(solution)/shard_map/psum | solution.py:304
  1424.4 33.1 %copy-start.20 = (f32[8,128]{1,0:T(8,128)S(1)}, f32[8,128]{1,0:T(8,128)}, u32[]{:S(2)}) copy-start(f32[8,128]{1,0:T(8,128)} %copy-done.19) | copy-start | bytes 12292
  (53 other events, 227.1 us)
Sparse Core Ops, SparseCore 0:
  9.9 86.9 all-gather.5
  98.8 39.7 all-gather.7
  140.4 101.0 all-gather.9
  243.3 101.0 all-gather.11
  715.5 38.3 reduce-scatter.9
  756.9 99.6 reduce-scatter.11
  859.8 99.6 reduce-scatter.13
  1375.1 82.3 reduce-scatter.7
  1460.8 24.3 reduce-scatter.15
  1487.7 162.3 all-reduce.19
where the time goes:
time: 1680 us; the launch traced here: 1670 us
  waiting for transfers between devices  492 us (29%)
  matrix products  447 us (27%)
  blocking collectives  350 us (21%)
  local copies, waits for them, and re-layouts  242 us (14%)
  other arithmetic  102 us (6%)
  between operations  18 us (1%)
    all_to_all x1, blocking collectives, on_device(): lax.all_to_all(for_sending(grad_stack), 'seq', split_axis=4, concat_axis=...  277 us
    all_to_all x1, waiting for transfers between devices, on_device(): lax.all_to_all(stacked, 'seq', split_axis=1, concat_axis=4, tiled=True)  155 us
    psum x1, waiting for transfers between devices, on_device(): lax.psum(part_qkv.astype(jnp.bfloat16), 'seq').astype(jnp.float32)  130 us
    all_to_all x1, waiting for transfers between devices, on_device(): lax.all_to_all(for_sending(mixed_items.reshape(local_heads, image_count,...  93.5 us
    dot_general x16, matrix products, attend_item(): jnp.einsum('qk,dk->dq', softmax_low, values, preferred_element_type=jnp.f...  64.5 us
    all_gather x1, waiting for transfers between devices, on_device(): lax.all_gather(w_qkv, 'fsdp', axis=0, tiled=True)  55.8 us
    dot_general x16, matrix products, attend_back(): jnp.einsum('qk,dq->dk', softmax_out.astype(jnp.bfloat16), grad_rows, pref...  42.4 us
    all_to_all x1, waiting for transfers between devices, on_device(): lax.all_to_all(grad_mixed, 'seq', split_axis=0, concat_axis=3, tiled=True)  37.8 us
  transfers between devices with their start and end apart: 13, of which 7 were waited for; matrix products, arithmetic and copies ran while one was open for 41% of the time, Pallas kernels for 0%

commit v1 on v0

--- a/solution.py
+++ b/solution.py
@@ -1,12 +1,29 @@
+import functools
 import jax
 import jax.numpy as jnp
 from jax import lax
 from jax.sharding import PartitionSpec as P
+from jax.lax import all_to_all, axis_size
 
 H = 16
 HD = 72
 epsilon = 1e-06
 wide_block = 1024
+
+
+def switch_the_state(obj, comm_axis):
+    return jnp.concatenate(
+        all_to_all(
+            jnp.stack(jnp.split(obj, axis_size(comm_axis), axis=4)),
+            axis_name=comm_axis,
+            split_axis=0,
+            concat_axis=0,
+        ),
+        axis=1,
+    )
+
+
+drive_steps_all = functools.partial(switch_the_state, comm_axis="seq")
 
 
 def for_sending(shard):
@@ -210,9 +227,7 @@
         (query_items, key_items, value_items, item_lengths, log_sums, grad_items),
     )
     grad_stack = jnp.stack([grad_q, grad_k, grad_v]).reshape(3, local_heads, image_count, HD, -1)
-    grad_projected = lax.all_to_all(
-        for_sending(grad_stack), "seq", split_axis=4, concat_axis=1, tiled=True
-    ).astype(grad_stack.dtype)
+    grad_projected = drive_steps_all(for_sending(grad_stack)).astype(grad_stack.dtype)
     column_scales = jnp.array([head_scale, 1.0, 1.0], jnp.float32)
     grad_qkv = (
         jnp.einsum(

time: 1680 us -> 1540 us (0.917)
  blocking collectives: 350 us -> 233 us
  local copies, waits for them, and re-layouts: 242 us -> 208 us
    all_to_all x1, blocking collectives: 277 us -> 158 us  [switch_the_state(): all_to_all(jnp.stack(jnp.split(obj, axis_size(comm_axis), axis=4)), axis_...]
    all_to_all x2 -> x0, local copies, waits for them, and re-layouts: 28.6 us -> none  [on_device(): lax.all_to_all(for_sending(grad_stack), 'seq', split_axis=4, concat_axis=...]
    while x35 -> x32, local copies, waits for them, and re-layouts: 49.7 us -> 32.1 us
  transfers between devices with their start and end apart: 13 -> 13, of which waited for: 7 -> 7; matrix products, arithmetic and copies ran while one was open for 41% -> 42% of each run, Pallas kernels for 0% -> 0%
where the time goes in v1:
time: 1540 us; the launch traced here: 1520 us
  waiting for transfers between devices  505 us (33%)
  matrix products  447 us (29%)
  blocking collectives  233 us (15%)
  local copies, waits for them, and re-layouts  208 us (14%)
  other arithmetic  95.1 us (6%)
  between operations  18.1 us (1%)
    all_to_all x1, blocking collectives, switch_the_state(): all_to_all(jnp.stack(jnp.split(obj, axis_size(comm_axis), axis=4)), axis_...  158 us
    all_to_all x1, waiting for transfers between devices, on_device(): lax.all_to_all(stacked, 'seq', split_axis=1, concat_axis=4, tiled=True)  155 us
    psum x1, waiting for transfers between devices, on_device(): lax.psum(part_qkv.astype(jnp.bfloat16), 'seq').astype(jnp.float32)  130 us
    all_to_all x1, waiting for transfers between devices, on_device(): lax.all_to_all(for_sending(mixed_items.reshape(local_heads, image_count,...  93.5 us
    dot_general x16, matrix products, attend_item(): jnp.einsum('qk,dk->dq', softmax_low, values, preferred_element_type=jnp.f...  64.5 us
    all_gather x1, waiting for transfers between devices, on_device(): lax.all_gather(w_qkv, 'fsdp', axis=0, tiled=True)  55.8 us
    dot_general x16, matrix products, attend_back(): jnp.einsum('qk,dq->dk', softmax_out.astype(jnp.bfloat16), grad_rows, pref...  42.4 us
    all_to_all x1, waiting for transfers between devices, on_device(): lax.all_to_all(grad_mixed, 'seq', split_axis=0, concat_axis=3, tiled=True)  37.9 us
  transfers between devices with their start and end apart: 13, of which 7 were waited for; matrix products, arithmetic and copies ran while one was open for 42% of the time, Pallas kernels for 0%

profile of v1, /device:TPU:0, one launch (start us, length us, event | category | flops | bytes accessed | tf_op | source)
XLA Modules:
  0.0 1522.3 jit_solution(12287948604341992781)
XLA Ops:
  13.0 18.5 %all-reduce.17 = (bf16[1152]{0:T(1024)(128)(2,1)S(1)}, bf16[1152]{0:T(1024)(128)(2,1)S(1)}, bf16[1152]{0:T(1024)(128)(2,1)S(1)}, bf16[1152]{0:T(1024)(128)(2,1)S...) all-reduce(bf16[1152]{0:T(1024)(128)(2,1)S(1)} %dynamic-update-slic, ...), channel_id=1, replica_groups=mesh['fsdp'=4,'seq'=8] {'fsdp'}, use_global_device_ids=true, to_apply=%add.1 | all-reduce | flops 10064 | bytes 40256
  41.2 55.8 %all-gather.6.cloned.1.call-done = bf16[1152,3456]{1,0:T(8,128)(2,1)} async-done(((bf16[288,3456]{1,0:T(8,128)(2,1)}), bf16[1152,3456]{1,0:T(8,128)(2,1)}) %all-gather.6.cloned.1.call-update) | async-done | bytes 7962640 | tf_op jit(solution)/shard_map/all_gather | solution.py:130
  96.9 11.6 copy.125
  108.5 12.5 convolution_bitcast_fusion.3
  133.9 155.1 %all-to-all-done = bf16[3,16,8,72,128]{4,3,0,2,1:T(8,128)(2,1)} async-done(((bf16[3,16,8,72,128]{4,3,0,2,1:T(8,128)(2,1)}), bf16[3,16,8,72,128]{4,3,0,2,1:T(8,128)(2,1)}, u32[]{:S(2)}, u32[]{:S(2)}) %all-to-all-start) | async-done | bytes 7077920 | tf_op jit(solution)/shard_map/all_to_all | solution.py:148
  289.0 7.7 fusion.123
  325.4 180.0 %while.26 = (s32[]{:T(128)}, bf16[16,72,1024]{2,1,0:T(8,128)(2,1)}, f32[16,1024]{1,0:T(8,128)}, bf16[16,72,1024]{2,1,0:T(8,128)(2,1)}, s32[16]{0:T(128)S(1)}, /*...) while((s32[]{:T(128)}, bf16[16,72,1024]{2,1,0:T(8,128)(2,1)}, ...), condition=%wide.region_5.6_spmd, body=%wide.region_2.5_spmd.sunk | while | flops 311500800 | bytes 29997196 | solution.py:155
  516.8 93.5 %all-to-all-done.1 = bf16[2,8,72,1024]{2,1,0,3:T(8,128)(2,1)} async-done(((bf16[2,8,72,1024]{2,1,0,3:T(8,128)(2,1)}), bf16[2,8,72,1024]{2,1,0,3:T(8,128)(2,1)}, u32[]{:S(2)}, u32[]{:S(2)}) %all-to-all-start.1) | async-done | bytes 2359328 | tf_op jit(solution)/shard_map/all_to_all | solution.py:158
  625.9 24.8 %multiply_convert_fusion.1 = (bf16[8,128,4304]{1,2,0:T(8,128)(2,1)}, f32[8,128,4304]{1,2,0:T(8,128)}) fusion(f32[4304]{0:T(1024)S(1)} %convert_element_type.186, bf16[1152,4304]{1,0:T(8,128)(2,1)} %all-gather.10.cloned.1.call-done, f32[8,128,1152]{2,1,0:T(8,128)} %copy-done.5, f32[1152]{0:T(1024)S(1)} %convert_element_type.184, ...), kind=kOutput, calls=%fused_computation.72 | convolution fusion | flops 10204381184 | bytes 41113408 | tf_op jit(solution)/shard_map/itd,df->itf/dot_general | solution.py:183
  650.7 32.5 %fusion.126 = (bf16[4304]{0:T(1024)(128)(2,1)}, bf16[8,128,4304]{1,2,0:T(8,128)(2,1)}) fusion(f32[8,128,4304]{1,2,0:T(8,128)} %get-tuple-element.199, f32[4304]{0:T(1024)S(1)} %convert_element_type.186, bf16[8,128,1152]{2,1,0:T(8,128)(2,1)} %param.34, bf16[4304,1152]{0,1:T(8,128)(2,1)} %all-gather.12.cloned.1.call-done), kind=kOutput, calls=%fused_computation.172 | convolution fusion | flops 10251366400 | bytes 38745312 | tf_op jit(solution)/shard_map/itd,fd->itf/dot_general | solution.py:204
  683.2 20.6 %multiply_reduce_fusion.1 = (bf16[1152]{0:T(1024)(128)(2,1)}, f32[8,128]{1,0:T(8,128)S(1)}, bf16[1152]{0:T(1024)(128)(2,1)}, f32[8,128,1152]{2,1,0:T(8,128)}) fusion(f32[8,128,1152]{2,1,0:T(8,128)S(1)} %bitcast.288, f32[8,128]{1,0:T(8,128)S(1)} %fusion.118, f32[8,128]{1,0:T(8,128)S(1)} %broadcast_multiply_fusion, f32[1152]{0:T(1024)S(1)} %convert_element_type.183, ...), kind=kOutput, calls=%fused_computation.117 | convolution fusion | flops 10163844096 | bytes 28189696 | tf_op jit(solution)/shard_map/itf,df->itd/dot_general | solution.py:209
  715.4 19.2 %fusion.54 = bf16[1152,4304]{1,0:T(8,128)(2,1)} fusion(bf16[8,128,4304]{1,2,0:T(8,128)(2,1)} %get-tuple-element.203, f32[8,128,1152]{2,1,0:T(8,128)} %copy-done.5, f32[1152]{0:T(1024)S(1)} %convert_element_type.184, f32[1152]{0:T(1024)S(1)} %convert_element_type.183, f32[8,128]{1,0:T(8,128)S(1)} %fusion.118, f32[8,128]{1,0:T(8,128)S(1)} %broadcast_multiply_fusion), kind=kOutput, calls=%fused_computation.63 | convolution fusion | flops 10165266432 | bytes 23467008 | tf_op jit(solution)/shard_map/itd,itf->df/dot_general | solution.py:207
  747.3 16.5 %fusion.55 = bf16[4304,1152]{0,1:T(8,128)(2,1)} fusion(bf16[8,128,4304]{1,2,0:T(8,128)(2,1)} %get-tuple-element.198, bf16[8,128,1152]{2,1,0:T(8,128)(2,1)S(1)} %copy-done.8), kind=kOutput, calls=%fused_computation.64 | convolution fusion | flops 10159368192 | bytes 21090304 | tf_op jit(solution)/shard_map/itf,itd->fd/dot_general | solution.py:202
  764.0 37.9 %all-to-all-done.2 = bf16[16,8,72,128]{3,2,1,0:T(8,128)(2,1)} async-done(((bf16[16,8,72,128]{3,2,1,0:T(8,128)(2,1)}), bf16[16,8,72,128]{3,2,1,0:T(8,128)(2,1)}, u32[]{:S(2)}, u32[]{:S(2)}) %all-to-all-start.2) | async-done | bytes 2359328 | tf_op jit(solution)/shard_map/all_to_all | solution.py:223
  811.3 220.8 %while.27 = (s32[]{:T(128)}, bf16[16,72,1024]{2,1,0:T(8,128)(2,1)S(1)}, bf16[16,72,1024]{2,1,0:T(8,128)(2,1)}, bf16[16,72,1024]{2,1,0:T(8,128)(2,1)}, bf16[16,72...) while((s32[]{:T(128)}, ...), condition=%wide.region_12.13_spmd, body=%wide.region_10.12_spmd.sunk | while | flops 767778816 | bytes 32969856 | solution.py:225
  1039.1 158.3 %all_to_all.53 = bf16[8,3,2,8,72,128]{5,4,2,3,1,0:T(8,128)(2,1)S(1)} all-to-all(bf16[8,3,2,8,72,128]{5,4,2,3,1,0:T(8,128)(2,1)S(1)} %copy.136), channel_id=1, replica_groups=mesh['fsdp'=4,'seq'=8] {'seq'}, dimensions={0} | all-to-all | bytes 14155776 | tf_op jit(solution)/shard_map/all_to_all | solution.py:16
  1202.8 13.9 fusion.63
  1216.7 11.6 copy.140
  1251.4 8.9 fusion.119
  1264.1 19.0 %all-reduce.16 = (bf16[1152]{0:T(1024)(128)(2,1)S(1)}, bf16[1152]{0:T(1024)(128)(2,1)S(1)}, bf16[1152]{0:T(1024)(128)(2,1)S(1)}, bf16[1152]{0:T(1024)(128)(2,1)S...) all-reduce(bf16[1152]{0:T(1024)(128)(2,1)S(1)} %dynamic-update-slic, ...), channel_id=1, replica_groups=mesh['fsdp'=4,'seq'=8] {'fsdp'}, use_global_device_ids=true, to_apply=%add.6 | all-reduce | flops 12368 | bytes 49472
  1283.7 28.1 %reduce-scatter.8.cloned.1.call-done = bf16[288,3456]{1,0:T(8,128)(2,1)} async-done(((bf16[1152,3456]{1,0:T(8,128)(2,1)}), bf16[288,3456]{1,0:T(8,128)(2,1)}) %reduce-scatter.8.cloned.1.call-update) | async-done | bytes 1990672 | tf_op jit(solution)/shard_map/reduce_scatter | solution.py:272
  1318.4 19.0 %fusion.94 = bf16[8,128,1152]{2,1,0:T(8,128)(2,1)} fusion(f32[8,128,1152]{2,1,0:T(8,128)} %copy-done.5, bf16[8,128,4304]{1,2,0:T(8,128)(2,1)} %get-tuple-element.198, bf16[4304,1152]{0,1:T(8,128)(2,1)} %all-gather.12.cloned.1.call-done, f32[1152]{0:T(1024)S(1)} %convert_element_type.188), kind=kOutput, calls=%fused_computation.123 | convolution fusion | flops 10157948928 | bytes 25813504 | tf_op jit(solution)/shard_map/itf,fd->itd/dot_general | solution.py:190
  1340.6 29.3 %all-reduce.14 = (bf16[288]{0:T(512)(128)(2,1)S(1)}, bf16[288]{0:T(512)(128)(2,1)S(1)}, bf16[2,288]{1,0:T(2,128)(2,1)S(1)}, bf16[288]{0:T(512)(128)(2,1)S(1)}, b...) all-reduce(bf16[288]{0:T(512)(128)(2,1)S(1)} %dynamic-slice.8, ...), channel_id=1, replica_groups=mesh['fsdp'=4,'seq'=8] {'seq'}, use_global_device_ids=true, to_apply=%region_17.18 | all-reduce | flops 3380 | bytes 13520 | tf_op jit(solution)/shard_map/psum | solution.py:317
  1374.6 130.0 %all-reduce.20.cloned.1.call-done = (bf16[288,3456]{1,0:T(8,128)(2,1)}, bf16[288,1152]{1,0:T(8,128)(2,1)}, bf16[288,4304]{1,0:T(8,128)(2,1)}, bf16[4304,288]{0,1:T(8,128)(2,1)}) async-done(((bf16[288,3456]{1,0:T(8,128)(2,1)}, bf16[288,1152]{1,0:T(8,128)(2,1)}, bf16[288,4304]{1,0:T(8,128)(2,1)}, bf16[4304,288]{0,1:T(8,128)(2,1)}), (bf16[288,3456]{1,0:T(8,128)(2,1)}, bf16[288,1152]{1,0:T(8,128)(2,1)}, ...) | async-done | bytes 7612432 | tf_op jit(solution)/shard_map/psum | solution.py:319
  (532 shorter events, 579.2 us)
Async XLA Ops:
  7.3 24.2 %copy-start.2 = (bf16[8,128,1152]{2,1,0:T(8,128)(2,1)S(1)}, bf16[8,128,1152]{2,1,0:T(8,128)(2,1)}, u32[]{:S(2)}) copy-start(bf16[8,128,1152]{2,1,0:T(8,128)(2,1)} %param.20) | copy-start | bytes 7077892
  7.3 26.0 %copy-start.34 = (bf16[2,288]{1,0:T(2,128)(2,1)S(1)}, bf16[2,288]{1,0:T(2,128)(2,1)}, u32[]{:S(2)}) copy-start(bf16[2,288]{1,0:T(2,128)(2,1)} %param.25) | copy-start | bytes 3460
  7.3 89.6 %all-gather.6.cloned.1.call-start = ((), (), s32[]{:S(2)}) async-start(), calls=%async_computation.9 | async-start | bytes 9953280 | tf_op jit(solution)/shard_map/all_gather | solution.py:130
  8.0 608.5 %all-gather.8.cloned.1.call-start = ((), (), s32[]{:S(2)}) async-start(), calls=%async_computation.10 | async-start | bytes 3317760 | tf_op jit(solution)/shard_map/all_gather | solution.py:132
  8.8 617.2 %all-gather.10.cloned.1.call-start = ((), (), s32[]{:S(2)}) async-start(), calls=%async_computation.11 | async-start | bytes 12533760 | tf_op jit(solution)/shard_map/all_gather | solution.py:174
  31.5 77.0 %copy-start.15 = (f32[1152]{0:T(1024)}, f32[1152]{0:T(1024)S(1)}, u32[]{:S(2)}) copy-start(f32[1152]{0:T(1024)S(1)} %convert_element_type.178) | copy-start | bytes 13828
  31.5 77.0 %copy-start.28 = (f32[1152]{0:T(1024)}, f32[1152]{0:T(1024)S(1)}, u32[]{:S(2)}) copy-start(f32[1152]{0:T(1024)S(1)} %convert_element_type.179) | copy-start | bytes 13828
  31.9 76.6 %copy-start.17 = (f32[8,128]{1,0:T(8,128)}, f32[8,128]{1,0:T(8,128)S(1)}, u32[]{:S(2)}) copy-start(f32[8,128]{1,0:T(8,128)S(1)} %broadcast_multiply_fusion.1) | copy-start | bytes 12292
  32.7 75.8 %copy-start.21 = (f32[8,128]{1,0:T(8,128)}, f32[8,128]{1,0:T(8,128)S(1)}, u32[]{:S(2)}) copy-start(f32[8,128]{1,0:T(8,128)S(1)} %fusion.117) | copy-start | bytes 12292
  128.3 160.7 %all-to-all-start = ((bf16[3,16,8,72,128]{4,3,0,2,1:T(8,128)(2,1)}), bf16[3,16,8,72,128]{4,3,0,2,1:T(8,128)(2,1)}, u32[]{:S(2)}, u32[]{:S(2)}) async-start(bf16[3,16,8,72,128]{4,3,0,2,1:T(8,128)(2,1)} %copy.127), calls=%async_computation | async-start | bytes 14155776 | tf_op jit(solution)/shard_map/all_to_all | solution.py:148
  133.3 517.4 %all-gather.12.cloned.1.call-start = ((), (), s32[]{:S(2)}) async-start(), calls=%async_computation.12 | async-start | bytes 12533760 | tf_op jit(solution)/shard_map/all_gather | solution.py:176
  511.7 98.6 %all-to-all-start.1 = ((bf16[2,8,72,1024]{2,1,0,3:T(8,128)(2,1)}), bf16[2,8,72,1024]{2,1,0,3:T(8,128)(2,1)}, u32[]{:S(2)}, u32[]{:S(2)}) async-start(bf16[2,8,72,1024]{2,1,0,3:T(8,128)(2,1)} %bitcast.289), calls=%async_computation.1 | async-start | bytes 8388608 | tf_op jit(solution)/shard_map/all_to_all | solution.py:158
  516.3 767.5 %reduce-scatter.10.cloned.1.call-start = ((), (), s32[]{:S(2)}) async-start(), calls=%async_computation.14 | async-start | bytes 3317760 | tf_op jit(solution)/shard_map/reduce_scatter | solution.py:278
  625.9 57.2 %slice-start.2 = ((s8[4718592]{0:T(1024)(128)(4,1)}), s8[524288]{0:T(1024)(128)(4,1)S(1)}, s32[]{:S(2)}) async-start(s8[4718592]{0:T(1024)(128)(4,1)} %bitcast.287), calls=%async_computation.21 | async-start | bytes 1048576
  650.7 32.5 %slice-start.3 = ((s8[4718592]{0:T(1024)(128)(4,1)}), s8[4194304]{0:T(1024)(128)(4,1)S(1)}, s32[]{:S(2)}) async-start(s8[4718592]{0:T(1024)(128)(4,1)} %bitcast.287), calls=%async_computation.22 | async-start | bytes 8388608
  715.3 568.4 %reduce-scatter.12.cloned.1.call-start = ((), (), s32[]{:S(2)}) async-start(), calls=%async_computation.15 | async-start | bytes 12533760 | tf_op jit(solution)/shard_map/reduce_scatter | solution.py:290
  742.9 59.0 %all-to-all-start.2 = ((bf16[16,8,72,128]{3,2,1,0:T(8,128)(2,1)}), bf16[16,8,72,128]{3,2,1,0:T(8,128)(2,1)}, u32[]{:S(2)}, u32[]{:S(2)}) async-start(bf16[16,8,72,128]{3,2,1,0:T(8,128)(2,1)} %copy.134), calls=%async_computation.2 | async-start | bytes 4718592 | tf_op jit(solution)/shard_map/all_to_all | solution.py:223
  747.2 536.5 %reduce-scatter.14.cloned.1.call-start = ((), (), s32[]{:S(2)}) async-start(), calls=%async_computation.16 | async-start | bytes 12533760 | tf_op jit(solution)/shard_map/reduce_scatter | solution.py:296
  763.8 548.0 %reduce-scatter.8.cloned.1.call-start = ((), (), s32[]{:S(2)}) async-start(), calls=%async_computation.13 | async-start | bytes 9953280 | tf_op jit(solution)/shard_map/reduce_scatter | solution.py:272
  1228.3 111.3 %reduce-scatter.16.cloned.1.call-start = ((), (), s32[]{:S(2)}) async-start(), calls=%async_computation.17 | async-start | bytes 368640
  1230.2 9.2 slice-start
  1251.3 8.9 copy-start.24
  1260.3 244.3 %all-reduce.20.cloned.1.call-start = ((), (), s32[]{:S(2)}) async-start(), calls=%async_computation.18 | async-start | bytes 15335424 | tf_op jit(solution)/shard_map/psum | solution.py:319
  1264.1 47.8 %copy-start.20 = (f32[8,128]{1,0:T(8,128)S(1)}, f32[8,128]{1,0:T(8,128)}, u32[]{:S(2)}) copy-start(f32[8,128]{1,0:T(8,128)} %copy-done.19) | copy-start | bytes 12292
  (55 other events, 192.2 us)
Sparse Core Ops, SparseCore 0:
  9.9 86.9 all-gather.5
  98.8 39.7 all-gather.7
  140.4 101.1 all-gather.9
  243.3 101.0 all-gather.11
  715.4 38.3 reduce-scatter.9
  756.9 99.6 reduce-scatter.11
  859.8 99.6 reduce-scatter.13
  1228.4 83.3 reduce-scatter.7
  1315.2 24.4 reduce-scatter.15
  1342.2 162.3 all-reduce.19
